TPU v7x, 32 devices: a whole 2x2x4 slice. The times are simulated.
32 devices in a mesh: row: 4 (over y, x), col: 8 (over z, core).
Axes of the slice: x: 2, y: 2, z: 4, core: 2. Of those that a mesh axis runs over, the one named last changes fastest.
Arguments:
- tiles: bfloat16 [1024, 256, 256], P(('row', 'col')), as said below
- tile_row: int32 [1024], P(('row', 'col')), may hold values from 0 to 31, as said below
- tile_col: int32 [1024], P(('row', 'col')), may hold values from 0 to 31, as said below
- label_class: int32 [8192], P(('row', 'col')), may hold values from -1 to 127, as said below
Outputs:
- scores: float32 [8192, 128], P(('row', 'col'))
- residual: float32 [8192, 128], P(('row', 'col'))
Inputs may be any that keep to these rules, and one draw needn't show every extreme that they name: `tiles`: Nonnegative. The tile of blocks (j, i) is the transpose of the tile of blocks (i, j); a tile on the diagonal is symmetric. No pair of blocks appears twice; the pair (j, i) is stored whenever (i, j) is. The device with row index r and col index c holds 32 tiles, all with tile_row // 8 == r and tile_col % 8 == c. `tile_col`: see tile_row. `label_class`: exactly 1024 nodes are labeled, and every class labels at least one node.
All inputs are finite; a program needn't handle non-finite values.
Results may differ from a plain program's by a relative error of at most 0.00062.
Values may be sent and summed in bfloat16 or wider, within the bound.
A program may use at most 64 MiB of HBM per device.

v0:
```python
import jax
import jax.numpy as jnp
from jax import lax
from jax.sharding import PartitionSpec as P

CLASSES = 128
ITERS = 3


def tile_apply(tiles, chosen, target, segment_count, blocks_in):
    gathered = blocks_in[chosen]
    einsum_form = "tab,tbk->tak"
    products = jnp.einsum(einsum_form, tiles, gathered, preferred_element_type=jnp.float32)
    return jax.ops.segment_sum(products, target, num_segments=segment_count)


def row_totals(tiles, target, segment_count):
    sums_axis = 2
    partial_sums = jnp.sum(tiles.astype(jnp.float32), axis=sums_axis)
    return jax.ops.segment_sum(partial_sums, target, num_segments=segment_count)


def shards(tiles, tile_row, tile_col, label_class):
    tile_size = tiles.shape[1]
    col_count = lax.axis_size("col")
    in_row = tile_row % col_count
    in_col = tile_col // col_count
    unlabeled = label_class < 0
    class_axis = jnp.arange(CLASSES, dtype=jnp.int32)
    label_blocks = lax.all_gather(label_class.reshape(1, tile_size), "row", axis=0, tiled=True)
    onehot = (label_blocks[:, :, None] == class_axis).astype(jnp.bfloat16)
    rhs_part = tile_apply(tiles, in_col, in_row, col_count, onehot)
    degree_part = row_totals(tiles, in_row, col_count)
    rhs_sum, degree_sum = (
        lax.psum_scatter(rhs_part, "col", scatter_dimension=0, tiled=True),
        lax.psum_scatter(degree_part, "col", scatter_dimension=0, tiled=True),
    )
    degree = degree_sum[0]
    rhs = jnp.where(unlabeled[:, None], rhs_sum[0], jnp.float32(0.0))
    solution = jnp.zeros((tile_size, CLASSES), jnp.float32)
    residual = rhs
    direction = rhs
    norm_now = lax.psum(jnp.sum(residual * residual, axis=0), ("row", "col"))
    for iteration in range(ITERS):
        panel = direction.astype(jnp.bfloat16).reshape(1, tile_size, CLASSES)
        panels = lax.all_gather(panel, "row", axis=0, tiled=True)
        partial_image = tile_apply(tiles, in_col, in_row, col_count, panels)
        mixed = lax.psum_scatter(partial_image, "col", scatter_dimension=0, tiled=True)[0]
        image = jnp.where(unlabeled[:, None], degree[:, None] * direction - mixed, direction)
        if iteration + 1 < ITERS:
            bending, crossed, energy = lax.psum(
                (
                    jnp.sum(direction * image, axis=0),
                    jnp.sum(residual * image, axis=0),
                    jnp.sum(image * image, axis=0),
                ),
                ("row", "col"),
            )
            alpha = norm_now / bending
            norm_next = norm_now - 2.0 * alpha * crossed + alpha * alpha * energy
            solution = solution + alpha * direction
            residual = residual - alpha * image
            direction = residual + norm_next / norm_now * direction
            norm_now = norm_next
        else:
            alpha = norm_now / lax.psum(jnp.sum(direction * image, axis=0), ("row", "col"))
            solution = solution + alpha * direction
            residual = residual - alpha * image
    return (8.0 * CLASSES * solution, residual)


def solution(mesh):
    placed = (
        P(("row", "col"), None, None),
        P(("row", "col")),
        P(("row", "col")),
        P(("row", "col")),
    )
    return jax.shard_map(
        shards,
        mesh=mesh,
        in_specs=placed,
        out_specs=(P(("row", "col"), None), P(("row", "col"), None)),
        check_vma=False,
    )
```

profile of v0, /device:TPU:0, one launch (start us, length us, event | category | flops | bytes accessed | tf_op | source)
XLA Modules:
  0.0 382.9 jit_solution(13755335169312421311)
XLA Ops:
  7.2 0.0 reduce-scatter.5.cloned.1.call-start
  7.2 0.7 and_select_fusion.1
  7.9 0.7 compare_select_fusion
  8.5 9.7 %all-gather.1 = s32[4,1,256]{2,1,0:T(1,128)S(1)} all-gather(s32[1,1,256]{2,1,0:T(1,128)} %bitcast.118), channel_id=2, replica_groups=mesh['row'=4,'col'=8] {'row'}, dimensions={0}, use_global_device_ids=true | all-gather | bytes 5120 | tf_op jit(solution)/shard_map/all_gather | solution.py:30
  18.2 0.2 iota_compare_fusion
  18.5 1.0 gather_fusion
  19.5 6.0 %convolution_bitcast_fusion = f32[32,256,128]{1,2,0:T(8,128)} fusion(bf16[32,256,256]{2,1,0:T(8,128)(2,1)} %param.4, pred[32,256,128]{2,1,0:T(32,128)(4,1)S(1)} %gather_fusion), kind=kOutput, calls=%fused_computation.10 | convolution fusion | flops 537919488 | bytes 9437184 | tf_op jit(solution)/shard_map/tab,tbk->tak/dot_general | solution.py:13
  25.5 5.6 %copy.22 = f32[32,256,128]{2,1,0:T(8,128)} copy(f32[32,256,128]{1,2,0:T(8,128)} %convolution_bitcast_fusion) | data formatting | bytes 8388608 | tf_op jit(solution)/shard_map/tab,tbk->tak/dot_general | solution.py:13
  31.1 0.1 broadcast.91.clone.1
  31.1 0.0 copy-start.7
  31.2 6.5 %scatter_fusion = f32[8,256,128]{2,1,0:T(8,128)S(1)} fusion(f32[8,256,128]{2,1,0:T(8,128)S(1)} %broadcast.91.clone.1, s32[32]{0:T(128)S(1)} %and_select_fusion.1, f32[32,256,128]{2,1,0:T(8,128)} %copy.22), kind=kCustom, calls=%fused_computation.4 | custom fusion | flops 1048576 | bytes 12583040 | tf_op jit(solution)/shard_map/scatter-add | solution.py:14
  37.6 0.0 copy-start.1
  37.6 1.0 copy-done.1
  38.6 0.0 reduce-scatter.5.cloned.1.call-update
  38.6 0.0 reduce-scatter.7.cloned.1.call-start
  38.7 0.0 copy-done.7
  38.7 32.9 %reduce-scatter.5.cloned.1.call-done = f32[1,256,128]{2,1,0:T(8,128)} async-done(((f32[8,256,128]{2,1,0:T(8,128)}), f32[1,256,128]{2,1,0:T(8,128)}) %reduce-scatter.5.cloned.1.call-update) | async-done | bytes 131088 | tf_op jit(solution)/shard_map/reduce_scatter | solution.py:35
  71.6 1.0 select_convert_fusion
  72.6 8.9 %all_gather.13 = bf16[4,256,128]{2,1,0:T(8,128)(2,1)S(1)} all-gather(bf16[1,256,128]{2,1,0:T(8,128)(2,1)S(1)} %select_convert_fusion), channel_id=1, replica_groups=mesh['row'=4,'col'=8] {'row'}, dimensions={0}, use_global_device_ids=true | all-gather | bytes 327680 | tf_op jit(solution)/shard_map/all_gather | solution.py:46
  81.5 1.0 gather_fusion.1
  82.5 5.6 %convolution_bitcast_fusion.3 = f32[32,256,128]{1,2,0:T(8,128)} fusion(bf16[32,256,128]{2,1,0:T(8,128)(2,1)S(1)} %gather_fusion.1, bf16[32,256,256]{2,1,0:T(8,128)(2,1)} %param.4), kind=kOutput, calls=%fused_computation.13 | convolution fusion | flops 536870912 | bytes 10485760 | tf_op jit(solution)/shard_map/tab,tbk->tak/dot_general | solution.py:13
  88.1 5.6 %copy.24 = f32[32,256,128]{2,1,0:T(8,128)} copy(f32[32,256,128]{1,2,0:T(8,128)} %convolution_bitcast_fusion.3) | data formatting | bytes 8388608 | tf_op jit(solution)/shard_map/tab,tbk->tak/dot_general | solution.py:13
  93.7 0.1 broadcast.91.clone.2
  93.8 6.5 %scatter_fusion.1 = f32[8,256,128]{2,1,0:T(8,128)S(1)} fusion(f32[8,256,128]{2,1,0:T(8,128)S(1)} %broadcast.91.clone.2, s32[32]{0:T(128)S(1)} %and_select_fusion.1, f32[32,256,128]{2,1,0:T(8,128)} %copy.24), kind=kCustom, calls=%fused_computation.6 | custom fusion | flops 1048576 | bytes 12583040 | tf_op jit(solution)/shard_map/scatter-add | solution.py:14
  100.2 0.0 copy-start.8
  100.3 1.0 copy-done.2
  101.2 0.0 reduce-scatter.7.cloned.1.call-update
  101.2 0.0 reduce-scatter.9.cloned.1.call-start
  101.3 3.3 convert_reduce_fusion
  104.6 0.7 scatter_custom_fusion.1
  105.4 0.0 copy-done.8
  105.4 0.6 dynamic-slice
  106.0 14.0 %all-reduce = f32[8,256]{1,0:T(8,128)S(1)} all-reduce(f32[8,256]{1,0:T(8,128)S(1)} %scatter_custom_fusion.1), channel_id=4, replica_groups=mesh['row'=4,'col'=8] {'col'}, use_global_device_ids=true, to_apply=%region_6.7.clone | all-reduce | flops 2048 | bytes 16384
  120.0 0.7 constant_dynamic-slice_fusion
  120.6 10.7 %reduce-scatter.7.cloned.1.call-done = f32[1,256,128]{2,1,0:T(8,128)} async-done(((f32[8,256,128]{2,1,0:T(8,128)}), f32[1,256,128]{2,1,0:T(8,128)}) %reduce-scatter.7.cloned.1.call-update) | async-done | bytes 131088 | tf_op jit(solution)/shard_map/reduce_scatter | solution.py:48
  131.3 0.0 copy-done.4
  131.3 1.1 multiply_reduce_fusion.5
  132.4 37.8 %all-reduce.2 = (f32[128]{0:T(128)S(1)}, f32[128]{0:T(128)S(1)}, f32[128]{0:T(128)S(1)}) all-reduce(f32[128]{0:T(128)S(1)} %get-tuple-element.6, f32[128]{0:T(128)S(1)} %get-tuple-element.7, f32[128]{0:T(128)S(1)} %get-tuple-element.5), channel_id=1, replica_groups=mesh['row'=4,'col'=8] {'row','col'}, use_global_device_ids=true, to_apply=%region_12.13 | all-reduce | flops 384 | bytes 3072 | tf_op jit(solution)/shard_map/psum | solution.py:51
  170.2 1.0 fusion.4
  171.3 10.3 %all_gather.14 = bf16[4,256,128]{2,1,0:T(8,128)(2,1)S(1)} all-gather(bf16[1,256,128]{2,1,0:T(8,128)(2,1)S(1)} %fusion.4), channel_id=1, replica_groups=mesh['row'=4,'col'=8] {'row'}, dimensions={0}, use_global_device_ids=true | all-gather | bytes 327680 | tf_op jit(solution)/shard_map/all_gather | solution.py:46
  181.5 1.0 gather_fusion.2
  182.5 5.6 %convolution_bitcast_fusion.2 = f32[32,256,128]{1,2,0:T(8,128)} fusion(bf16[32,256,128]{2,1,0:T(8,128)(2,1)S(1)} %gather_fusion.2, bf16[32,256,256]{2,1,0:T(8,128)(2,1)} %param.4), kind=kOutput, calls=%fused_computation.12 | convolution fusion | flops 536870912 | bytes 10485760 | tf_op jit(solution)/shard_map/tab,tbk->tak/dot_general | solution.py:13
  188.1 5.6 %copy.26 = f32[32,256,128]{2,1,0:T(8,128)} copy(f32[32,256,128]{1,2,0:T(8,128)} %convolution_bitcast_fusion.2) | data formatting | bytes 8388608 | tf_op jit(solution)/shard_map/tab,tbk->tak/dot_general | solution.py:13
  193.7 0.1 broadcast.91.clone
  193.8 6.5 %scatter_fusion.2 = f32[8,256,128]{2,1,0:T(8,128)S(1)} fusion(f32[8,256,128]{2,1,0:T(8,128)S(1)} %broadcast.91.clone, s32[32]{0:T(128)S(1)} %and_select_fusion.1, f32[32,256,128]{2,1,0:T(8,128)} %copy.26), kind=kCustom, calls=%fused_computation.7 | custom fusion | flops 1048576 | bytes 12583040 | tf_op jit(solution)/shard_map/scatter-add | solution.py:14
  200.2 1.0 copy-done.3
  201.2 0.0 reduce-scatter.9.cloned.1.call-update
  201.2 0.0 reduce-scatter.11.cloned.1.call-start
  201.3 32.3 %reduce-scatter.9.cloned.1.call-done = f32[1,256,128]{2,1,0:T(8,128)} async-done(((f32[8,256,128]{2,1,0:T(8,128)}), f32[1,256,128]{2,1,0:T(8,128)}) %reduce-scatter.9.cloned.1.call-update) | async-done | bytes 131088 | tf_op jit(solution)/shard_map/reduce_scatter | solution.py:48
  233.6 1.1 multiply_reduce_fusion.2
  234.7 37.7 %all-reduce.1 = (f32[128]{0:T(128)S(1)}, f32[128]{0:T(128)S(1)}, f32[128]{0:T(128)S(1)}) all-reduce(f32[128]{0:T(128)S(1)} %get-tuple-element.3, f32[128]{0:T(128)S(1)} %get-tuple-element.4, f32[128]{0:T(128)S(1)} %get-tuple-element.2), channel_id=1, replica_groups=mesh['row'=4,'col'=8] {'row','col'}, use_global_device_ids=true, to_apply=%region_20.21 | all-reduce | flops 384 | bytes 3072 | tf_op jit(solution)/shard_map/psum | solution.py:51
  272.4 1.1 add_convert_fusion
  273.5 10.1 %all_gather.15 = bf16[4,256,128]{2,1,0:T(8,128)(2,1)S(1)} all-gather(bf16[1,256,128]{2,1,0:T(8,128)(2,1)S(1)} %add_convert_fusion), channel_id=1, replica_groups=mesh['row'=4,'col'=8] {'row'}, dimensions={0}, use_global_device_ids=true | all-gather | bytes 327680 | tf_op jit(solution)/shard_map/all_gather | solution.py:46
  283.6 1.0 gather_fusion.3
  284.5 5.6 %convolution_bitcast_fusion.1 = f32[32,256,128]{1,2,0:T(8,128)} fusion(bf16[32,256,128]{2,1,0:T(8,128)(2,1)S(1)} %gather_fusion.3, bf16[32,256,256]{2,1,0:T(8,128)(2,1)} %param.4), kind=kOutput, calls=%fused_computation.11 | convolution fusion | flops 536870912 | bytes 10485760 | tf_op jit(solution)/shard_map/tab,tbk->tak/dot_general | solution.py:13
  290.2 5.6 %copy.28 = f32[32,256,128]{2,1,0:T(8,128)} copy(f32[32,256,128]{1,2,0:T(8,128)} %convolution_bitcast_fusion.1) | data formatting | bytes 8388608 | tf_op jit(solution)/shard_map/tab,tbk->tak/dot_general | solution.py:13
  295.7 0.1 broadcast.91
  295.8 6.5 %scatter_fusion.3 = f32[8,256,128]{2,1,0:T(8,128)S(1)} fusion(f32[8,256,128]{2,1,0:T(8,128)S(1)} %broadcast.91, s32[32]{0:T(128)S(1)} %and_select_fusion.1, f32[32,256,128]{2,1,0:T(8,128)} %copy.28), kind=kCustom, calls=%fused_computation.8 | custom fusion | flops 1048576 | bytes 12583040 | tf_op jit(solution)/shard_map/scatter-add | solution.py:14
  302.3 1.0 copy-done
  303.3 0.0 reduce-scatter.11.cloned.1.call-update
  303.3 32.3 %reduce-scatter.11.cloned.1.call-done = f32[1,256,128]{2,1,0:T(8,128)} async-done(((f32[8,256,128]{2,1,0:T(8,128)}), f32[1,256,128]{2,1,0:T(8,128)}) %reduce-scatter.11.cloned.1.call-update) | async-done | bytes 131088 | tf_op jit(solution)/shard_map/reduce_scatter | solution.py:48
  335.6 1.1 multiply_reduce_fusion
  336.7 37.8 %psum.58 = f32[128]{0:T(128)S(1)} all-reduce(f32[128]{0:T(128)S(1)} %multiply_reduce_fusion), channel_id=1, replica_groups=mesh['row'=4,'col'=8] {'row','col'}, use_global_device_ids=true, to_apply=%region_24.25 | all-reduce | flops 128 | bytes 1024 | tf_op jit(solution)/shard_map/psum | solution.py:66
  374.6 1.8 multiply_subtract_fusion
  (14 shorter events, 0.1 us)
Async XLA Ops:
  7.2 64.4 %reduce-scatter.5.cloned.1.call-start = ((), (), s32[]{:S(2)}) async-start(), calls=%async_computation.4 | async-start | bytes 1179648 | tf_op jit(solution)/shard_map/reduce_scatter | solution.py:35
  31.1 7.5 %copy-start.7 = (s32[256]{0:T(256)S(1)}, s32[256]{0:T(256)}, u32[]{:S(2)}) copy-start(s32[256]{0:T(256)} %param.7) | copy-start | bytes 3076
  37.6 1.0 copy-start.1
  38.6 92.7 %reduce-scatter.7.cloned.1.call-start = ((), (), s32[]{:S(2)}) async-start(), calls=%async_computation.5 | async-start | bytes 1179648 | tf_op jit(solution)/shard_map/reduce_scatter | solution.py:48
  100.2 1.0 copy-start.2
  100.2 5.2 %copy-start.8 = (u32[32]{0:T(128)S(1)}, u32[32]{0:T(128)}, u32[]{:S(2)}) copy-start(u32[32]{0:T(128)} %constant.42) | copy-start | bytes 388
  100.2 31.1 %copy-start.4 = (f32[1,256,128]{2,1,0:T(8,128)S(1)}, f32[1,256,128]{2,1,0:T(8,128)}, u32[]{:S(2)}) copy-start(f32[1,256,128]{2,1,0:T(8,128)} %reduce-scatter.5.cloned.1.call-done) | copy-start | bytes 393220
  101.2 132.4 %reduce-scatter.9.cloned.1.call-start = ((), (), s32[]{:S(2)}) async-start(), calls=%async_computation.6 | async-start | bytes 1179648 | tf_op jit(solution)/shard_map/reduce_scatter | solution.py:48
  193.7 39.9 %copy-start.5 = (f32[1,256,128]{2,1,0:T(8,128)S(1)}, f32[1,256,128]{2,1,0:T(8,128)}, u32[]{:S(2)}) copy-start(f32[1,256,128]{2,1,0:T(8,128)} %reduce-scatter.7.cloned.1.call-done) | copy-start | bytes 393220
  200.2 1.0 copy-start.3
  201.2 134.4 %reduce-scatter.11.cloned.1.call-start = ((), (), s32[]{:S(2)}) async-start(), calls=%async_computation.7 | async-start | bytes 1179648 | tf_op jit(solution)/shard_map/reduce_scatter | solution.py:48
  295.8 39.8 %copy-start.6 = (f32[1,256,128]{2,1,0:T(8,128)S(1)}, f32[1,256,128]{2,1,0:T(8,128)}, u32[]{:S(2)}) copy-start(f32[1,256,128]{2,1,0:T(8,128)} %reduce-scatter.9.cloned.1.call-done) | copy-start | bytes 393220
  302.3 1.0 copy-start
Sparse Core Ops, SparseCore 0:
  38.8 32.7 reduce-scatter.4
  101.4 29.8 reduce-scatter.6
  201.4 32.1 reduce-scatter.8
  303.4 32.1 reduce-scatter.10
where the time goes:
time: 385 us; the launch traced here: 383 us
  blocking collectives  166 us (43%)
  waiting for transfers between devices  108 us (28%)
  other arithmetic  39.6 us (10%)
  local copies, waits for them, and re-layouts  31.6 us (8%)
  matrix products  22.9 us (6%)
  between operations  14 us (4%)
    psum x2, blocking collectives, shards(): lax.psum((jnp.sum(direction * image, axis=0), jnp.sum(residual * image, a...  75.6 us
    reduce_scatter x3, waiting for transfers between devices, shards(): lax.psum_scatter(partial_image, 'col', scatter_dimension=0, tiled=True)[0]  75.3 us
    psum x1, blocking collectives, shards(): lax.psum(jnp.sum(direction * image, axis=0), ('row', 'col'))  37.8 us
    reduce_scatter x1, waiting for transfers between devices, shards(): lax.psum_scatter(rhs_part, 'col', scatter_dimension=0, tiled=True)  32.9 us
    all_gather x3, blocking collectives, shards(): panels = lax.all_gather(panel, 'row', axis=0, tiled=True)  29.3 us
    scatter-add x4, other arithmetic, tile_apply(): return jax.ops.segment_sum(products, target, num_segments=segment_count)  25.8 us
    dot_general x4, matrix products, tile_apply(): jnp.einsum(einsum_form, tiles, gathered, preferred_element_type=jnp.float32)  22.9 us
    dot_general x4, local copies, waits for them, and re-layouts, tile_apply(): jnp.einsum(einsum_form, tiles, gathered, preferred_element_type=jnp.float32)  22.3 us
  transfers between devices with their start and end apart: 4, of which 4 were waited for; matrix products, arithmetic and copies ran while one was open for 1% of the time, Pallas kernels for 0%

commit v1 on v0

v1 whole, which is shorter than its diff:
```python
import functools

import jax
import jax.numpy as jnp
from jax import lax
from jax.experimental import pallas as pl
from jax.experimental.pallas import tpu as pltpu
from jax.sharding import PartitionSpec as P

CLASSES = 128
ITERS = 3
PAD = 16
DEG = 8
UNROLL = 32
PARTS = 4


def each(count, body, unroll):
    if unroll:
        for n in range(count):
            body(n)
    else:
        def step(n, carry):
            body(n)
            return carry
        lax.fori_loop(0, count, step, 0)


def flip(index, mask):
    bit = 1
    result = index
    while bit <= mask:
        if mask & bit:
            result = result + bit * (1 - 2 * lax.rem(lax.div(index, bit), 2))
        bit *= 2
    return result


def kernel(
    R, C, pos, label_ref, tiles_hbm, x_out, r_out,
    tiles, lab, ag0, ag, acc0, acc, rs0, rs, st_ag, st_row, st_rs,
    degree, unlabeled, direction, image,
    tile_sem, lab_send, lab_recv, ag_send, ag_recv, st_send, st_recv,
    str_send, str_recv, rs_send, rs_recv,
):
    T, B = tiles_hbm.shape[0], tiles_hbm.shape[1]
    Z = C // 2
    K = CLASSES
    unroll = R * C <= UNROLL
    row, col = lax.axis_index("row"), lax.axis_index("col")
    core = lax.rem(col, 2)
    peer = col + 1 - 2 * core
    pow2_z = Z & (Z - 1) == 0
    pow2_r = R & (R - 1) == 0
    assert pow2_z and pow2_r

    def col_partner(m):
        return flip(col, m)

    def row_partner(m):
        return flip(row, m)

    step = -(-T // PARTS)
    tile_copies = []
    for p in range(PARTS):
        lo, hi = p * step, min(T, (p + 1) * step)
        if lo < hi:
            cp = pltpu.make_async_copy(
                tiles_hbm.at[pl.ds(lo, hi - lo)], tiles.at[pl.ds(lo, hi - lo)], tile_sem.at[p]
            )
            cp.start()
            tile_copies.append(cp)
    if tiles.shape[0] > T:
        tiles[T] = jnp.zeros((B, B), jnp.bfloat16)

    barrier = pltpu.get_barrier_semaphore()
    for m in range(1, C):
        pl.semaphore_signal(
            barrier, inc=1, device_id={"col": col_partner(m)}, device_id_type=pl.DeviceIdType.MESH
        )
    for m in range(1, R):
        pl.semaphore_signal(
            barrier, inc=1, device_id={"row": row_partner(m)}, device_id_type=pl.DeviceIdType.MESH
        )
    mine = label_ref[...]
    lab[col] = jnp.broadcast_to(mine, (8, B))
    pl.semaphore_wait(barrier, C - 1 + R - 1)

    sent = []

    def send(src, dst, send_sem, recv_sem, where):
        cp = pltpu.make_async_remote_copy(
            src_ref=src, dst_ref=dst, send_sem=send_sem, recv_sem=recv_sem,
            device_id=where, device_id_type=pl.DeviceIdType.MESH,
        )
        cp.start()
        sent.append(cp)

    def arrive(dst, recv_sem):
        pltpu.make_async_remote_copy(
            src_ref=dst, dst_ref=dst, send_sem=tile_sem.at[0], recv_sem=recv_sem,
            device_id={"col": peer}, device_id_type=pl.DeviceIdType.MESH,
        ).wait_recv()

    def tile_at(source, k):
        return tiles[pos[source * R + k]]

    def scatter(stage, total, slots, k_body):
        for m in range(R - 1, 0, -1):
            k = row_partner(m)
            k_body(k)
            send(total.at[k], slots.at[m - 1], rs_send.at[stage, m], rs_recv.at[stage, m],
                 {"row": k})
        k_body(row)
        result = total[row]
        for m in range(1, R):
            arrive(slots.at[m - 1], rs_recv.at[stage, m])
            result = result + slots[m - 1]
        return result

    def stats_start(s, rows):
        padded = jnp.concatenate(rows + [jnp.zeros((8 - len(rows), K), jnp.float32)], axis=0)
        st_ag[s, col] = padded
        for m in range(1, C):
            send(st_ag.at[s, col], st_ag.at[s, col], st_send.at[s, m], st_recv.at[s, col],
                 {"col": col_partner(m)})

    def stats_middle(s):
        for m in range(1, C):
            c = col_partner(m)
            arrive(st_ag.at[s, c], st_recv.at[s, c])
        st_row[s] = jnp.sum(st_ag[s], axis=0)
        for m in range(1, R):
            send(st_row.at[s], st_rs.at[s, row], str_send.at[s, m], str_recv.at[s, row],
                 {"row": row_partner(m)})
        st_rs[s, row] = st_row[s]

    def stats_end(s):
        for m in range(1, R):
            k = row_partner(m)
            arrive(st_rs.at[s, k], str_recv.at[s, k])
        return jnp.sum(st_rs[s], axis=0)

    for m in range(1, C):
        send(lab.at[col], lab.at[col], lab_send.at[m], lab_recv.at[col], {"col": col_partner(m)})
    class_axis = lax.broadcasted_iota(jnp.int32, (K, B), 0)
    ones = jnp.ones((PAD, B), jnp.bfloat16)

    def encode(c):
        hot = jnp.where(lab[c][0:1] == class_axis, 1.0, 0.0).astype(jnp.bfloat16)
        ag0[c] = jnp.concatenate([hot, ones], axis=0)

    encode(col)
    unlabeled[...] = jnp.where(jnp.broadcast_to(mine, (K, B)) < 0, 1.0, 0.0).T
    for m in range(1, C):
        c = col_partner(m)
        arrive(lab.at[c], lab_recv.at[c])
        encode(c)
    for cp in tile_copies:
        cp.wait()

    def first_products(k):
        if unroll:
            value = jnp.zeros((K + PAD, B), jnp.float32)
            for c in range(C):
                value = value + jnp.dot(ag0[c], tile_at(c, k), preferred_element_type=jnp.float32)
        else:
            value = lax.fori_loop(
                0, C,
                lambda c, v: v + jnp.dot(ag0[c], tile_at(c, k), preferred_element_type=jnp.float32),
                jnp.zeros((K + PAD, B), jnp.float32),
            )
        acc0[k] = value[: K + DEG]

    total = scatter(0, acc0, rs0, first_products)
    free = unlabeled[...] > 0.0
    degree[...] = jnp.broadcast_to(total[K : K + 1], (K, B)).T
    rhs = jnp.where(free, total[:K].T, 0.0)

    def inner(a, b):
        return jnp.sum(a * b, axis=0, keepdims=True)

    def operator(stage, v, first_norm):
        s = stage - 1
        ag[s, col] = v.T.astype(jnp.bfloat16)
        own = ag.at[s, col]
        for o in range(1, Z):
            send(own, own, ag_send.at[s, o], ag_recv.at[s, col], {"col": col_partner(2 * o)})
        send(own, own, ag_send.at[s, 0], ag_recv.at[s, col], {"col": peer})

        def add(c, first=False):
            panel = ag[s, c]

            def one(k):
                value = jnp.dot(panel, tile_at(c, k), preferred_element_type=jnp.float32)
                acc[s, k] = value if first else acc[s, k] + value
            each(R, one, unroll)

        add(col, first=True)
        arrive(ag.at[s, peer], ag_recv.at[s, peer])
        add(peer)
        for o in range(1, Z):
            c = col_partner(2 * o)
            block = ag.at[s, c]
            arrive(block, ag_recv.at[s, c])
            send(block, block, ag_send.at[s, Z + o], ag_recv.at[s, c], {"col": peer})
            add(c)
        if first_norm:
            stats_middle(ITERS)
        for o in range(1, Z):
            c = col_partner(2 * o + 1)
            arrive(ag.at[s, c], ag_recv.at[s, c])

        def finish(k):
            value = acc[s, k]
            for o in range(1, Z):
                c = col_partner(2 * o + 1)
                value = value + jnp.dot(ag[s, c], tile_at(c, k), preferred_element_type=jnp.float32)
            acc[s, k] = value

        mixed = scatter(stage, acc.at[s], rs.at[s], finish).T
        product = jnp.where(unlabeled[...] > 0.0, degree[...] * v - mixed, v)
        return product

    x_out[...] = jnp.zeros((B, K), jnp.float32)
    r_out[...] = rhs
    direction[...] = rhs
    stats_start(ITERS, [inner(rhs, rhs)])
    for iteration in range(ITERS):
        product = operator(iteration + 1, direction[...], iteration == 0)
        image[...] = product
        d, r = direction[...], r_out[...]
        if iteration == 0:
            norm = stats_end(ITERS)[0:1]
        last = iteration + 1 == ITERS
        stats_start(
            iteration, [inner(d, product)] + ([] if last else [inner(r, product), inner(product, product)])
        )
        stats_middle(iteration)
        sums = stats_end(iteration)
        alpha = norm / sums[0:1]
        d, i = direction[...], image[...]
        r = r_out[...] - alpha * i
        r_out[...] = r
        x = x_out[...] + alpha * d
        if last:
            x_out[...] = (8.0 * K) * x
        else:
            norm_next = norm - 2.0 * alpha * sums[1:2] + alpha * alpha * sums[2:3]
            direction[...] = r + norm_next / norm * d
            x_out[...] = x
            norm = norm_next
    for cp in sent:
        cp.wait_send()


def solution(mesh):
    R, C = mesh.shape["row"], mesh.shape["col"]

    def shards(tiles, tile_row, tile_col, label_class):
        T, B = tiles.shape[0], tiles.shape[1]
        K = CLASSES
        place = (tile_row % C) * R + tile_col // C
        slot = jnp.arange(R * C, dtype=jnp.int32)
        index = jnp.arange(T, dtype=jnp.int32)
        pos = T - jnp.sum(jnp.where(place[None, :] == slot[:, None], T - index[None, :], 0), axis=1)
        held = T if T == R * C else T + 1
        f32, bf16 = jnp.float32, jnp.bfloat16
        dma = pltpu.SemaphoreType.DMA
        vmem = pl.BlockSpec(memory_space=pltpu.VMEM)
        node = pltpu.VMEM((B, K), f32)
        return pl.pallas_call(
            functools.partial(kernel, R, C),
            out_shape=(jax.ShapeDtypeStruct((B, K), f32), jax.ShapeDtypeStruct((B, K), f32)),
            in_specs=[
                pl.BlockSpec(memory_space=pltpu.SMEM),
                vmem,
                pl.BlockSpec(memory_space=pl.ANY),
            ],
            out_specs=(vmem, vmem),
            scratch_shapes=[
                pltpu.VMEM((held, B, B), bf16),
                pltpu.VMEM((C, 8, B), jnp.int32),
                pltpu.VMEM((C, K + PAD, B), bf16),
                pltpu.VMEM((ITERS, C, K, B), bf16),
                pltpu.VMEM((R, K + DEG, B), f32),
                pltpu.VMEM((ITERS, R, K, B), f32),
                pltpu.VMEM((R - 1, K + DEG, B), f32),
                pltpu.VMEM((ITERS, R - 1, K, B), f32),
                pltpu.VMEM((ITERS + 1, C, 8, K), f32),
                pltpu.VMEM((ITERS + 1, 8, K), f32),
                pltpu.VMEM((ITERS + 1, R, 8, K), f32),
                node, node, node, node,
                dma((PARTS,)),
                dma((C,)), dma((C,)),
                dma((ITERS, C)), dma((ITERS, C)),
                dma((ITERS + 1, C)), dma((ITERS + 1, C)),
                dma((ITERS + 1, R)), dma((ITERS + 1, R)),
                dma((ITERS + 1, R)), dma((ITERS + 1, R)),
            ],
            compiler_params=pltpu.CompilerParams(
                collective_id=0, has_side_effects=True, vmem_limit_bytes=48 * 1024 * 1024
            ),
        )(pos.astype(jnp.int32), label_class.reshape(1, B), tiles)

    placed = (P(("row", "col"), None, None),) + (P(("row", "col")),) * 3
    return jax.shard_map(
        shards,
        mesh=mesh,
        in_specs=placed,
        out_specs=(P(("row", "col"), None), P(("row", "col"), None)),
        check_vma=False,
    )
```

time: 385 us -> 93.8 us (0.24)
  blocking collectives: 166 us -> 0 us
  waiting for transfers between devices: 108 us -> 0 us
  Pallas kernels: 0 us -> 88 us
  other arithmetic: 39.6 us -> 0.8 us
  local copies, waits for them, and re-layouts: 31.6 us -> 4.18 us
  matrix products: 22.9 us -> 0 us
  between operations: 14 us -> 0.65 us
    psum x3 -> x0, blocking collectives: 113 us -> none  [the longest x2 75.6 us: shards(): lax.psum((jnp.sum(direction * image, axis=0), jnp.sum(residual * image, a...]
    reduce_scatter x4 -> x0, waiting for transfers between devices: 108 us -> none  [the longest x3 75.3 us: shards(): lax.psum_scatter(partial_image, 'col', scatter_dimension=0, tiled=True)[0]]
    pallas_call x0 -> x1, Pallas kernels: none -> 88 us  [shards(): pl.pallas_call(functools.partial(kernel, R, C), out_shape=(jax.ShapeDtype...]
    all_gather x4 -> x0, blocking collectives: 39 us -> none  [the longest x3 29.3 us: shards(): panels = lax.all_gather(panel, 'row', axis=0, tiled=True)]
    scatter-add x5 -> x0, other arithmetic: 26.6 us -> none  [the longest x4 25.8 us: tile_apply(): return jax.ops.segment_sum(products, target, num_segments=segment_count)]
    dot_general x4 -> x0, matrix products: 22.9 us -> none  [tile_apply(): jnp.einsum(einsum_form, tiles, gathered, preferred_element_type=jnp.float32)]
    dot_general x4 -> x0, local copies, waits for them, and re-layouts: 22.3 us -> none  [tile_apply(): jnp.einsum(einsum_form, tiles, gathered, preferred_element_type=jnp.float32)]
    unnamed x1 -> x0, blocking collectives: 14 us -> none
  transfers between devices with their start and end apart: 4 -> 0, of which waited for: 4 -> 0; matrix products, arithmetic and copies ran while one was open for 1% -> 0% of each run, Pallas kernels for 0% -> 0%
where the time goes in v1:
time: 93.8 us; the launch traced here: 93.6 us
  Pallas kernels  88 us (94%)
  local copies, waits for them, and re-layouts  4.18 us (4%)
    pallas_call x1, Pallas kernels, shards(): pl.pallas_call(functools.partial(kernel, R, C), out_shape=(jax.ShapeDtype...  88 us
    unnamed x6, local copies, waits for them, and re-layouts  4.18 us

profile of v1, /device:TPU:0, one launch (start us, length us, event | category | flops | bytes accessed | tf_op | source)
XLA Modules:
  0.0 93.6 jit_solution(12409379704373845582)
XLA Ops:
  0.6 0.7 fusion.1
  1.3 0.1 select_reduce_fusion
  1.4 0.0 copy-start
  1.4 2.2 %copy-done = bf16[32,256,256]{2,1,0:T(8,128)(2,1)S(1)} copy-done((bf16[32,256,256]{2,1,0:T(8,128)(2,1)S(1)}, bf16[32,256,256]{2,1,0:T(8,128)(2,1)}, u32[]{:S(2)}) %copy-start) | copy-done | bytes 4194328
  3.6 0.0 copy-start.1
  3.6 0.7 copy-done.1
  4.3 88.0 %shard_map.59 = (f32[256,128]{1,0:T(8,128)S(1)}, f32[256,128]{1,0:T(8,128)S(1)}) custom-call(s32[32]{0:T(128)S(1)} %broadcast_subtract_fusion.pos, s32[1,256]{1,0:T(1,128)S(1)} %bitcast.1, bf16[32,256,256]{2,1,0:T(8,128)(2,1)S(1)} %copy-done), custom_call_target="tpu_custom_call" | custom-call | tf_op jit(solution)/shard_map/pallas_call | solution.py:272
  92.3 0.7 copy.8
  92.9 0.7 copy.9
  (1 shorter events, 0.0 us)
Async XLA Ops:
  1.4 2.2 %copy-start = (bf16[32,256,256]{2,1,0:T(8,128)(2,1)S(1)}, bf16[32,256,256]{2,1,0:T(8,128)(2,1)}, u32[]{:S(2)}) copy-start(bf16[32,256,256]{2,1,0:T(8,128)(2,1)} %tiles_hbm.1) | copy-start | bytes 12582916
  3.6 0.7 copy-start.1

commit v2 on v1

v2 whole, which is shorter than its diff:
```python
import functools

import jax
import jax.numpy as jnp
from jax import lax
from jax.experimental import pallas as pl
from jax.experimental.pallas import tpu as pltpu
from jax.sharding import PartitionSpec as P

CLASSES = 128
ITERS = 3
PAD = 16
DEG = 8
UNROLL = 32
PARTS = 4


def each(count, body, unroll):
    if unroll:
        for n in range(count):
            body(n)
    else:
        def step(n, carry):
            body(n)
            return carry
        lax.fori_loop(0, count, step, 0)


def flip(index, mask):
    bit = 1
    result = index
    while bit <= mask:
        if mask & bit:
            result = result + bit * (1 - 2 * lax.rem(lax.div(index, bit), 2))
        bit *= 2
    return result


def kernel(
    R, C, pos, label_ref, tiles_hbm, x_out, r_out,
    tiles, lab, ag0, ag, acc0a, acc0b, acc, rs0a, rs0b, rs, st_ag, st_row, st_rs,
    degree, direction, image, residual, answer,
    tile_sem, lab_send, lab_recv, ag_send, ag_recv, st_send, st_recv,
    str_send, str_recv, rs_send, rs_recv,
):
    T, B = tiles_hbm.shape[0], tiles_hbm.shape[1]
    Z = C // 2
    K, H = CLASSES, CLASSES // 2
    unroll = R * C <= UNROLL
    row, col = lax.axis_index("row"), lax.axis_index("col")
    core = lax.rem(col, 2)
    peer = col + 1 - 2 * core
    pow2_z = Z & (Z - 1) == 0
    pow2_r = R & (R - 1) == 0
    assert pow2_z and pow2_r

    def col_partner(m):
        return flip(col, m)

    def row_partner(m):
        return flip(row, m)

    step = -(-T // PARTS)
    tile_copies = []
    for p in range(PARTS):
        lo, hi = p * step, min(T, (p + 1) * step)
        if lo < hi:
            cp = pltpu.make_async_copy(
                tiles_hbm.at[pl.ds(lo, hi - lo)], tiles.at[pl.ds(lo, hi - lo)], tile_sem.at[p]
            )
            cp.start()
            tile_copies.append(cp)
    if tiles.shape[0] > T:
        tiles[T] = jnp.zeros((B, B), jnp.bfloat16)

    barrier = pltpu.get_barrier_semaphore()
    for m in range(1, C):
        pl.semaphore_signal(
            barrier, inc=1, device_id={"col": col_partner(m)}, device_id_type=pl.DeviceIdType.MESH
        )
    for m in range(1, R):
        pl.semaphore_signal(
            barrier, inc=1, device_id={"row": row_partner(m)}, device_id_type=pl.DeviceIdType.MESH
        )
    mine = label_ref[...]
    lab[col] = jnp.broadcast_to(mine, (8, B))
    pl.semaphore_wait(barrier, C - 1 + R - 1)

    sent = []

    def send(src, dst, send_sem, recv_sem, where):
        cp = pltpu.make_async_remote_copy(
            src_ref=src, dst_ref=dst, send_sem=send_sem, recv_sem=recv_sem,
            device_id=where, device_id_type=pl.DeviceIdType.MESH,
        )
        cp.start()
        sent.append(cp)

    def arrive(dst, recv_sem):
        pltpu.make_async_remote_copy(
            src_ref=dst, dst_ref=dst, send_sem=tile_sem.at[0], recv_sem=recv_sem,
            device_id={"col": peer}, device_id_type=pl.DeviceIdType.MESH,
        ).wait_recv()

    def tile_at(source, k):
        return tiles[pos[source * R + k]]

    def scatter_start(t, total, slots, k_body):
        for m in range(R - 1, 0, -1):
            k = row_partner(m)
            k_body(k)
            send(total.at[k], slots.at[m - 1], rs_send.at[t, m], rs_recv.at[t, m], {"row": k})
        k_body(row)

    def scatter_end(t, total, slots):
        result = total[row]
        for m in range(1, R):
            arrive(slots.at[m - 1], rs_recv.at[t, m])
            result = result + slots[m - 1]
        return result

    def inner(a, b):
        product = a * b
        folded = product[:, :K]
        for lane in range(K, B, K):
            folded = folded + product[:, lane : lane + K]
        padded = jnp.concatenate([folded, jnp.zeros((K - H, K), jnp.float32)], axis=0)
        return jnp.sum(padded.T, axis=0, keepdims=True)

    def spread(values):
        square = jnp.broadcast_to(values, (K, K)).T[:H]
        return jnp.concatenate([square] * (B // K), axis=1)

    def stats_start(t, rows):
        st_ag[t, col] = jnp.concatenate(rows + [jnp.zeros((8 - len(rows), K), jnp.float32)], axis=0)
        for m in range(1, C):
            send(st_ag.at[t, col], st_ag.at[t, col], st_send.at[t, m], st_recv.at[t, col],
                 {"col": col_partner(m)})

    def stats_middle(t):
        for m in range(1, C):
            c = col_partner(m)
            arrive(st_ag.at[t, c], st_recv.at[t, c])
        st_row[t] = jnp.sum(st_ag[t], axis=0)
        for m in range(1, R):
            send(st_row.at[t], st_rs.at[t, row], str_send.at[t, m], str_recv.at[t, row],
                 {"row": row_partner(m)})
        st_rs[t, row] = st_row[t]

    def stats_end(t):
        for m in range(1, R):
            k = row_partner(m)
            arrive(st_rs.at[t, k], str_recv.at[t, k])
        return jnp.sum(st_rs[t], axis=0)

    for m in range(1, C):
        send(lab.at[col], lab.at[col], lab_send.at[m], lab_recv.at[col], {"col": col_partner(m)})
    class_axis = lax.broadcasted_iota(jnp.int32, (K, B), 0)
    ones = jnp.ones((PAD, B), jnp.bfloat16)

    def encode(c):
        hot = jnp.where(lab[c][0:1] == class_axis, 1.0, 0.0).astype(jnp.bfloat16)
        ag0[c] = jnp.concatenate([hot[:H], ones, hot[H:]], axis=0)

    encode(col)
    for m in range(1, C):
        c = col_partner(m)
        arrive(lab.at[c], lab_recv.at[c])
        encode(c)
    for cp in tile_copies:
        cp.wait()
    free = jnp.broadcast_to(mine, (H, B)) < 0

    def chain(h):
        lo, rows_in = (0, H + PAD) if h == 0 else (H + PAD, H)
        total, slots = (acc0a, rs0a) if h == 0 else (acc0b, rs0b)
        keep = total.shape[1]

        def first_products(k):
            def one(c, value):
                return value + jnp.dot(
                    ag0[c, lo : lo + rows_in], tile_at(c, k), preferred_element_type=jnp.float32
                )
            value = jnp.zeros((rows_in, B), jnp.float32)
            if unroll:
                for c in range(C):
                    value = one(c, value)
            else:
                value = lax.fori_loop(0, C, one, value)
            total[k] = value[:keep]

        scatter_start(h, total, slots, first_products)
        yield
        value = scatter_end(h, total, slots)
        if h == 0:
            degree[...] = value[H : H + DEG]
        rhs = jnp.where(free, value[:H], 0.0)
        answer[h] = jnp.zeros((H, B), jnp.float32)
        residual[h] = rhs
        direction[h] = rhs
        start = 2 * ITERS + h
        for iteration in range(ITERS):
            s = 2 * iteration + h
            last = iteration + 1 == ITERS
            ag[s, col] = direction[h].astype(jnp.bfloat16)
            own = ag.at[s, col]
            for o in range(1, Z):
                send(own, own, ag_send.at[s, o], ag_recv.at[s, col], {"col": col_partner(2 * o)})
            send(own, own, ag_send.at[s, 0], ag_recv.at[s, col], {"col": peer})
            if iteration == 0:
                stats_start(start, [inner(rhs, rhs)])

            def add(c, first=False):
                panel = ag[s, c]

                def one(k):
                    part = jnp.dot(panel, tile_at(c, k), preferred_element_type=jnp.float32)
                    acc[s, k] = part if first else acc[s, k] + part
                each(R, one, unroll)

            add(col, first=True)
            yield
            arrive(ag.at[s, peer], ag_recv.at[s, peer])
            add(peer)
            for o in range(1, Z):
                c = col_partner(2 * o)
                block = ag.at[s, c]
                arrive(block, ag_recv.at[s, c])
                send(block, block, ag_send.at[s, Z + o], ag_recv.at[s, c], {"col": peer})
                add(c)
            if iteration == 0:
                stats_middle(start)
            yield
            for o in range(1, Z):
                c = col_partner(2 * o + 1)
                arrive(ag.at[s, c], ag_recv.at[s, c])

            def finish(k):
                part = acc[s, k]
                for o in range(1, Z):
                    c = col_partner(2 * o + 1)
                    part = part + jnp.dot(ag[s, c], tile_at(c, k), preferred_element_type=jnp.float32)
                acc[s, k] = part

            scatter_start(2 + s, acc.at[s], rs.at[s], finish)
            yield
            mixed = scatter_end(2 + s, acc.at[s], rs.at[s])
            d, r = direction[h], residual[h]
            i = jnp.where(free, degree[0:1] * d - mixed, d)
            image[h] = i
            stats_start(s, [inner(d, i)] + ([] if last else [inner(r, i), inner(i, i)]))
            yield
            stats_middle(s)
            yield
            if iteration == 0:
                norm = stats_end(start)[0:1]
            sums = stats_end(s)
            alpha = norm / sums[0:1]
            wide = spread(alpha)
            d = direction[h]
            r = residual[h] - wide * image[h]
            x = answer[h] + wide * d
            if last:
                x_out[:, h * H : (h + 1) * H] = ((8.0 * K) * x).T
                r_out[:, h * H : (h + 1) * H] = r.T
            else:
                norm_next = norm - 2.0 * alpha * sums[1:2] + alpha * alpha * sums[2:3]
                direction[h] = r + spread(norm_next / norm) * d
                residual[h] = r
                answer[h] = x
                norm = norm_next

    running = [chain(0), chain(1)]
    while running:
        for one in list(running):
            if next(one, running) is running:
                running.remove(one)
    for cp in sent:
        cp.wait_send()


def solution(mesh):
    R, C = mesh.shape["row"], mesh.shape["col"]

    def shards(tiles, tile_row, tile_col, label_class):
        T, B = tiles.shape[0], tiles.shape[1]
        K, H = CLASSES, CLASSES // 2
        place = (tile_row % C) * R + tile_col // C
        slot = jnp.arange(R * C, dtype=jnp.int32)
        index = jnp.arange(T, dtype=jnp.int32)
        held = T if T == R * C else T + 1
        pos = jnp.max(jnp.where(place[None, :] == slot[:, None], T - index[None, :], T + 1 - held), axis=1)
        pos = T - pos
        f32, bf16 = jnp.float32, jnp.bfloat16
        dma = pltpu.SemaphoreType.DMA
        vmem = pl.BlockSpec(memory_space=pltpu.VMEM)
        node = pltpu.VMEM((2, H, B), f32)
        return pl.pallas_call(
            functools.partial(kernel, R, C),
            out_shape=(jax.ShapeDtypeStruct((B, K), f32), jax.ShapeDtypeStruct((B, K), f32)),
            in_specs=[
                pl.BlockSpec(memory_space=pltpu.SMEM),
                vmem,
                pl.BlockSpec(memory_space=pl.ANY),
            ],
            out_specs=(vmem, vmem),
            scratch_shapes=[
                pltpu.VMEM((held, B, B), bf16),
                pltpu.VMEM((C, 8, B), jnp.int32),
                pltpu.VMEM((C, K + PAD, B), bf16),
                pltpu.VMEM((2 * ITERS, C, H, B), bf16),
                pltpu.VMEM((R, H + DEG, B), f32),
                pltpu.VMEM((R, H, B), f32),
                pltpu.VMEM((2 * ITERS, R, H, B), f32),
                pltpu.VMEM((R - 1, H + DEG, B), f32),
                pltpu.VMEM((R - 1, H, B), f32),
                pltpu.VMEM((2 * ITERS, R - 1, H, B), f32),
                pltpu.VMEM((2 * ITERS + 2, C, 8, K), f32),
                pltpu.VMEM((2 * ITERS + 2, 8, K), f32),
                pltpu.VMEM((2 * ITERS + 2, R, 8, K), f32),
                pltpu.VMEM((DEG, B), f32),
                node, node, node, node,
                dma((PARTS,)),
                dma((C,)), dma((C,)),
                dma((2 * ITERS, C)), dma((2 * ITERS, C)),
                dma((2 * ITERS + 2, C)), dma((2 * ITERS + 2, C)),
                dma((2 * ITERS + 2, R)), dma((2 * ITERS + 2, R)),
                dma((2 * ITERS + 2, R)), dma((2 * ITERS + 2, R)),
            ],
            compiler_params=pltpu.CompilerParams(
                collective_id=0, has_side_effects=True, vmem_limit_bytes=63 * 1024 * 1024
            ),
        )(pos.astype(jnp.int32), label_class.reshape(1, B), tiles)

    placed = (P(("row", "col"), None, None),) + (P(("row", "col")),) * 3
    return jax.shard_map(
        shards,
        mesh=mesh,
        in_specs=placed,
        out_specs=(P(("row", "col"), None), P(("row", "col"), None)),
        check_vma=False,
    )
```

time: 93.8 us -> 90.2 us (0.962)
  Pallas kernels: 88 us -> 84.9 us
  local copies, waits for them, and re-layouts: 4.18 us -> 3.14 us
    pallas_call x1, Pallas kernels: 88 us -> 84.9 us  [shards(): pl.pallas_call(functools.partial(kernel, R, C), out_shape=(jax.ShapeDtype...]
    unnamed x6 -> x2, local copies, waits for them, and re-layouts: 4.18 us -> 3.14 us
where the time goes in v2:
time: 90.2 us; the launch traced here: 90 us
  Pallas kernels  84.9 us (94%)
  local copies, waits for them, and re-layouts  3.14 us (3%)
  other arithmetic  1.32 us (1%)
    pallas_call x1, Pallas kernels, shards(): pl.pallas_call(functools.partial(kernel, R, C), out_shape=(jax.ShapeDtype...  84.9 us
    unnamed x2, local copies, waits for them, and re-layouts  3.14 us

profile of v2, /device:TPU:0, one launch (start us, length us, event | category | flops | bytes accessed | tf_op | source)
XLA Modules:
  0.0 90.0 jit_solution(2646302820275178186)
XLA Ops:
  0.6 0.7 fusion.1
  1.3 0.1 select_reduce_fusion
  1.4 0.5 broadcast_subtract_fusion.pos
  1.9 84.9 %shard_map.59 = (f32[256,128]{1,0:T(8,128)}, f32[256,128]{1,0:T(8,128)}) custom-call(s32[32]{0:T(128)} %broadcast_subtract_fusion.pos, s32[1,256]{1,0:T(1,128)} %bitcast.1, bf16[32,256,256]{2,1,0:T(8,128)(2,1)} %tiles_hbm.1), custom_call_target="tpu_custom_call" | custom-call | tf_op jit(solution)/shard_map/pallas_call | solution.py:298
  86.9 1.6 %copy.8 = f32[256,128]{1,0:T(8,128)} copy(f32[256,128]{1,0:T(8,128)} %get-tuple-element.6) | data formatting | bytes 262144
  88.4 1.6 %copy.9 = f32[256,128]{1,0:T(8,128)} copy(f32[256,128]{1,0:T(8,128)} %get-tuple-element.7) | data formatting | bytes 262144
